TPU v7x, 32 devices: a whole 2x2x4 slice. The times are simulated.
32 devices in a mesh: lon: 8 (over y, x, core), lat: 4 (over z).
Axes of the slice: x: 2, y: 2, z: 4, core: 2. Of those that a mesh axis runs over, the one named last changes fastest.
Arguments:
- fields: bfloat16 [32, 256, 256], P('lat', 'lon'), may hold values from -6 to 6
- norm_lon: float32 [256], replicated, may hold values from 0.25 to 1.75
- query_lon: bfloat16 [256, 256], replicated, may hold values from -0.375 to 0.375
- key_lon: bfloat16 [256, 256], replicated, may hold values from -0.375 to 0.375
- value_lon: bfloat16 [256, 256], replicated, may hold values from -0.375 to 0.375
- out_lon: bfloat16 [256, 256], replicated, may hold values from -0.375 to 0.375
- temp_lon: float32 [8], replicated, may hold values from 0.5 to 12
- bias_lon: float32 [8], replicated, may hold values from -2 to 2
- norm_lat: float32 [256], replicated, may hold values from 0.25 to 1.75
- query_lat: bfloat16 [256, 256], replicated, may hold values from -0.375 to 0.375
- key_lat: bfloat16 [256, 256], replicated, may hold values from -0.375 to 0.375
- value_lat: bfloat16 [256, 256], replicated, may hold values from -0.375 to 0.375
- out_lat: bfloat16 [256, 256], replicated, may hold values from -0.375 to 0.375
- temp_lat: float32 [8], replicated, may hold values from 0.5 to 12
- bias_lat: float32 [8], replicated, may hold values from -4 to 0
- norm_mlp: float32 [256], replicated, may hold values from 0.25 to 1.75
- w_gate: bfloat16 [256, 1024], replicated, may hold values from -0.375 to 0.375
- w_up: bfloat16 [256, 1024], replicated, may hold values from -0.375 to 0.375
- w_down: bfloat16 [1024, 256], replicated, may hold values from -0.1875 to 0.1875
Outputs:
- updated: bfloat16 [32, 256, 256], P('lat', 'lon')
All inputs are finite; a program needn't handle non-finite values.
Results may differ from a plain program's by a relative error of at most 0.018.
The roundings to bfloat16 on the way count: a program that leaves them out, or rounds other values in their place, can miss the bound.
Values may be sent and summed in bfloat16 or wider, within the bound.
A program may use at most 64 MiB of HBM per device.

v0:
```python
import math

import jax
import jax.numpy as jnp
import functools
import numpy as np
from jax import lax
from jax.experimental import pallas as pl
from jax.experimental.pallas import tpu as pltpu
from jax.sharding import PartitionSpec as P


def normalize(values, gain):
    factor = lax.rsqrt(jnp.mean(values * values, axis=-1, keepdims=True) + 1e-06)
    return (values * factor * gain).astype(jnp.bfloat16)


def project(values, weight):
    return jnp.dot(values, weight, preferred_element_type=jnp.float32).astype(jnp.bfloat16)


def attend_lat(queries, keys, values, temp, bias):
    count, cols, depth = queries.shape
    heads = temp.shape[0]
    size = depth // heads
    qh = queries.reshape(count, cols, heads, size)
    kh = keys.reshape(count, cols, heads, size)
    vh = values.reshape(count, cols, heads, size)
    scores = jnp.einsum("ichd,jchd->chij", qh, kh, preferred_element_type=jnp.float32)
    place = jnp.arange(count, dtype=jnp.int32)
    spread = jnp.abs(place[:, None] - place[None, :]).astype(jnp.float32) / count
    scores = (
        scores * (temp / math.sqrt(size))[None, :, None, None]
        + bias[None, :, None, None] * spread[None, None]
    )
    expo = jnp.exp(scores - jnp.max(scores, axis=-1, keepdims=True))
    denom = jnp.sum(expo, axis=-1)
    mixed = jnp.einsum(
        "chij,jchd->ichd", expo.astype(jnp.bfloat16), vh, preferred_element_type=jnp.float32
    )
    mixed = mixed / jnp.transpose(denom, (2, 0, 1))[..., None]
    return mixed.astype(jnp.bfloat16).reshape(count, cols, depth)


def body(
    fields,
    norm_lon,
    query_lon,
    key_lon,
    value_lon,
    out_lon,
    temp_lon,
    bias_lon,
    norm_lat,
    query_lat,
    key_lat,
    value_lat,
    out_lat,
    temp_lat,
    bias_lat,
    norm_mlp,
    w_gate,
    w_up,
    w_down,
):
    rows, width, depth = fields.shape
    heads = temp_lon.shape[0]
    size = depth // heads
    total_lon = width * lax.axis_size("lon")
    resid = fields.astype(jnp.float32)
    normed = normalize(resid, norm_lon)
    scale_lon = temp_lon / math.sqrt(size)
    query_place = lax.axis_index("lon") * width + jnp.arange(width, dtype=jnp.int32)
    queries = project(normed, query_lon).reshape(rows, width, heads, size)
    piece = lax.all_gather(normed, "lon", axis=1, tiled=True)
    keys = project(piece, key_lon)
    count = keys.shape[1]
    key_place = jnp.arange(count, dtype=jnp.int32)
    angle = (query_place[:, None] - key_place[None, :]).astype(jnp.float32) * (
        2.0 * math.pi / total_lon
    )
    wave = jnp.cos(angle)

    def one_row(items):
        query_row, key_row, value_row, peak, total, accum = items
        key_heads = key_row.reshape(count, heads, size)
        value_heads = value_row.reshape(count, heads, size)
        scores = jnp.einsum(
            "ihd,jhd->hij", query_row, key_heads, preferred_element_type=jnp.float32
        )
        scores = scores * scale_lon[:, None, None] + bias_lon[:, None, None] * wave[None]
        fresh = jnp.maximum(peak, jnp.max(scores, axis=-1))
        shrink = jnp.exp(peak - fresh)
        expo = jnp.exp(scores - fresh[..., None])
        total = total * shrink + jnp.sum(expo, axis=-1)
        mixed = jnp.einsum(
            "hij,jhd->ihd",
            expo.astype(jnp.bfloat16),
            value_heads,
            preferred_element_type=jnp.float32,
        )
        accum = accum.reshape(width, heads, size) * jnp.transpose(shrink)[:, :, None] + mixed
        return (fresh, total, accum.reshape(width, depth))

    peak = jnp.full((rows, heads, width), -1e30, jnp.float32)
    total = jnp.zeros((rows, heads, width), jnp.float32)
    accum = jnp.zeros((rows, width, depth), jnp.float32)
    peak, total, accum = lax.map(
        one_row, (queries, keys, project(piece, value_lon), peak, total, accum)
    )
    attended = accum.reshape(rows, width, heads, size) / jnp.transpose(total, (0, 2, 1))[..., None]
    attended = attended.astype(jnp.bfloat16).reshape(rows, width, depth)
    first = resid + jnp.dot(attended, out_lon, preferred_element_type=jnp.float32)
    normed_lat = normalize(first, norm_lat)
    query_col = project(normed_lat, query_lat)
    key_col = project(normed_lat, key_lat)
    value_col = project(normed_lat, value_lat)
    query_col, key_col, value_col = (
        lax.all_to_all(query_col, "lat", split_axis=1, concat_axis=0, tiled=True),
        lax.all_to_all(key_col, "lat", split_axis=1, concat_axis=0, tiled=True),
        lax.all_to_all(value_col, "lat", split_axis=1, concat_axis=0, tiled=True),
    )
    mixed_lat = attend_lat(query_col, key_col, value_col, temp_lat, bias_lat)
    returned = lax.all_to_all(mixed_lat, "lat", split_axis=0, concat_axis=1, tiled=True)
    second = first + jnp.dot(returned, out_lat, preferred_element_type=jnp.float32)
    normed_mlp = normalize(second, norm_mlp)
    gate = jnp.dot(normed_mlp, w_gate, preferred_element_type=jnp.float32)
    upper = jnp.dot(normed_mlp, w_up, preferred_element_type=jnp.float32)
    hidden = (jax.nn.silu(gate) * upper).astype(jnp.bfloat16)
    return (second + jnp.dot(hidden, w_down, preferred_element_type=jnp.float32)).astype(
        jnp.bfloat16
    )


NT = (((1,), (1,)), ((), ()))
MESH = pl.DeviceIdType.MESH
F32 = jnp.float32
BF16 = jnp.bfloat16


def mm(a, b):
    return jnp.dot(a, b, preferred_element_type=F32)


def mm_nt(a, b):
    return lax.dot_general(a, b, NT, preferred_element_type=F32)


def iota(shape, dim):
    return lax.broadcasted_iota(jnp.int32, shape, dim)


def heads_t(keys, queries_t, values_t, temp, bias, table, mask, heads, size):
    outs = []
    for h in range(heads):
        part = slice(h * size, (h + 1) * size)
        scores = mm(keys[:, part], queries_t[part, :])
        scores = scores * (temp[:, h:h + 1] / math.sqrt(size)) + bias[:, h:h + 1] * table
        if mask is not None:
            scores = scores + mask
        expo = jnp.exp(scores - jnp.max(scores, axis=0, keepdims=True))
        denom = jnp.sum(expo, axis=0, keepdims=True)
        outs.append(mm(values_t[part, :], expo.astype(BF16)) / denom)
    return jnp.concatenate(outs, axis=0).astype(BF16)


def block_kernel(
    n_lon, n_lat, rows, width, depth, heads,
    fields_h, gain_lon_h, gain_lat_h, gain_mlp_h, temp_lon_h, bias_lon_h, temp_lat_h, bias_lat_h,
    wave_h, wq1_h, wk1_h, wv1_h, wo1_h, wq2_h, wk2_h, wv2_h, wo2_h, wg_h, wu_h, wd_h,
    out,
    fields, gain_lon, gain_lat, gain_mlp, temp_lon, bias_lon, temp_lat, bias_lat,
    wave, wq1, wk1, wv1, wo1, wq2, wk2, wv2, wo2, wg, wu, wd,
    norm_out, norm_in, field_out, field_in, att_out, att_in, upd_out,
    local_sem, s1, r1, s2, r2, s3, r3, s4, r4,
):
    me_lon = lax.axis_index("lon")
    me_lat = lax.axis_index("lat")
    total = n_lon * n_lat
    me = me_lon * n_lat + me_lat
    size = depth // heads
    cols = width // n_lat
    count = n_lat * rows
    cells = rows * width

    barrier = pltpu.get_barrier_semaphore()

    def greet(step, carry):
        peer = lax.rem(me + step, total)
        pl.semaphore_signal(
            barrier, inc=1, device_id=(peer // n_lat, lax.rem(peer, n_lat)), device_id_type=MESH
        )
        return carry

    lax.fori_loop(1, total, greet, 0)

    loads = [
        pltpu.make_async_copy(src, dst, local_sem.at[i])
        for i, (src, dst) in enumerate(
            [(fields_h, fields), (gain_lon_h, gain_lon), (wq1_h, wq1), (wk1_h, wk1), (wv1_h, wv1), (wave_h, wave), (wo1_h, wo1), (wq2_h, wq2),
             (wk2_h, wk2), (wv2_h, wv2), (wo2_h, wo2), (wg_h, wg), (wu_h, wu), (wd_h, wd),
             (gain_lat_h, gain_lat), (gain_mlp_h, gain_mlp), (temp_lon_h, temp_lon), (bias_lon_h, bias_lon),
             (temp_lat_h, temp_lat), (bias_lat_h, bias_lat)]
        )
    ]
    for load in loads:
        load.start()

    for load in loads[:2]:
        load.wait()
    wide = fields[...].astype(F32)
    norm_out[...] = normalize(wide, gain_lon[...][None])
    pieces = wide.reshape(rows, n_lat, cols, depth).astype(BF16)
    for a in range(n_lat):
        field_out[a] = pieces[:, a]

    pl.semaphore_wait(barrier, total - 1)

    def send_norm(step):
        peer = lax.rem(me_lon + step, n_lon)
        return pltpu.make_async_remote_copy(
            src_ref=norm_out.at[peer], dst_ref=norm_in.at[me_lon], send_sem=s1.at[step],
            recv_sem=r1.at[step], device_id=(peer, me_lat), device_id_type=MESH,
        )

    def lat_copy(step, src, dst, ssem, rsem):
        peer = lax.rem(me_lat + step, n_lat)
        return pltpu.make_async_remote_copy(
            src_ref=src.at[peer], dst_ref=dst.at[me_lat], send_sem=ssem.at[step],
            recv_sem=rsem.at[step], device_id=(me_lon, peer), device_id_type=MESH,
        )

    sends1 = [send_norm(step) for step in range(1, n_lon)]
    for copy in sends1:
        copy.start()
    sends2 = [lat_copy(step, field_out, field_in, s2, r2) for step in range(1, n_lat)]
    for copy in sends2:
        copy.start()
    norm_in[pl.ds(me_lon, 1)] = norm_out[pl.ds(me_lon, 1)]
    field_in[pl.ds(me_lat, 1)] = field_out[pl.ds(me_lat, 1)]

    shape = (cells, cells)
    lanes = iota(shape, 1)
    subs = iota(shape, 0)
    to_cols = (lax.rem(subs, count) * cols + subs // count == lanes).astype(F32).astype(BF16)
    from_cols = (lax.rem(lanes, count) * cols + lanes // count == subs).astype(F32).astype(BF16)
    eye = (lanes == subs).astype(F32).astype(BF16)
    half = cells // 2
    hs, hl = iota((half, half), 0), iota((half, half), 1)
    spread = jnp.abs(lax.rem(hs, count) - lax.rem(hl, count)).astype(F32) / count
    mask = jnp.where(hs // count == hl // count, 0.0, -1e30).astype(F32)

    early = loads[2:6] + loads[16:18]
    for load in early:
        load.wait()
    wq_t = wq1[...].T
    wv_t = wv1[...].T

    for copy in sends1:
        copy.wait_recv()

    nlon = n_lon * width
    normed = norm_in[...].reshape(nlon, depth)
    keys = mm(normed, wk1[...]).astype(BF16)
    queries_t = mm_nt(wq_t, normed).astype(BF16)
    values_t = mm_nt(wv_t, normed).astype(BF16)
    my_row = me_lat * rows + me_lon

    def att_copy(peer, row):
        return pltpu.make_async_remote_copy(
            src_ref=att_out.at[peer], dst_ref=att_in.at[row], send_sem=s3.at[peer],
            recv_sem=r3.at[row], device_id=(peer // n_lat, lax.rem(peer, n_lat)),
            device_id_type=MESH,
        )

    batch = min(nlon, 128)
    group = batch // cols
    for start in range(0, nlon, batch):
        span = slice(start, start + batch)
        att_t = heads_t(keys, queries_t[:, span], values_t, temp_lon, bias_lon, wave[:, span], None, heads, size)
        att = mm_nt(eye[:batch, :batch], att_t)
        first_peer = start // cols
        att_out[first_peer:first_peer + group] = att.reshape(group, cols, depth).astype(BF16)

        def start_att(step, carry, first_peer=first_peer):
            peer = first_peer + lax.rem(me + step, group)

            @pl.when(peer != me)
            def _():
                att_copy(peer, my_row).start()

            return carry

        lax.fori_loop(0, group, start_att, 0)
    att_in[pl.ds(my_row, 1)] = att_out[pl.ds(me, 1)]

    def wait_att(step, carry):
        att_copy(lax.rem(me + step, total), lax.rem(my_row + step, count)).wait_recv()
        return carry

    def wait_att_send(step, carry):
        att_copy(lax.rem(me + step, total), my_row).wait_send()
        return carry

    for load in loads[6:16] + loads[18:]:
        load.wait()
    wq2_t = wq2[...].T
    wv2_t = wv2[...].T
    for copy in sends2:
        copy.wait_recv()
    lax.fori_loop(1, total, wait_att, 0)

    resid = field_in[...].astype(F32).reshape(cells, depth)
    attended = att_in[...].astype(F32).reshape(cells, depth).astype(BF16)
    first = resid + mm(attended, wo1[...])
    normed = mm(to_cols, normalize(first, gain_lat[...])).astype(BF16)
    keys = mm(normed, wk2[...]).astype(BF16)
    queries_t = mm_nt(wq2_t, normed).astype(BF16)
    values_t = mm_nt(wv2_t, normed).astype(BF16)
    parts = []
    for part in (slice(0, half), slice(half, cells)):
        parts.append(
            heads_t(keys[part], queries_t[:, part], values_t[:, part], temp_lat, bias_lat,
                    spread, mask, heads, size)
        )
    att_t = jnp.concatenate(parts, axis=1)
    attended = mm_nt(from_cols, att_t).astype(BF16)
    second = first + mm(attended, wo2[...])
    normed = normalize(second, gain_mlp[...])
    ff = wg.shape[1]
    step_ff = min(ff, 256)
    for f in range(0, ff, step_ff):
        gate = mm(normed, wg[:, f:f + step_ff])
        upper = mm(normed, wu[:, f:f + step_ff])
        hidden = (gate / (1.0 + jnp.exp(-gate)) * upper).astype(BF16)
        second = second + mm(hidden, wd[f:f + step_ff, :])
    upd_out[...] = second.reshape(n_lat, rows, cols, depth).astype(BF16)

    def upd_copy(step):
        peer = lax.rem(me_lat + step, n_lat)
        return pltpu.make_async_remote_copy(
            src_ref=upd_out.at[peer], dst_ref=out.at[:, pl.ds(pl.multiple_of(me_lat * cols, cols), cols), :],
            send_sem=s4.at[step], recv_sem=r4.at[step], device_id=(me_lon, peer), device_id_type=MESH,
        )

    sends4 = [upd_copy(step) for step in range(1, n_lat)]
    for copy in sends4:
        copy.start()
    own = pltpu.make_async_copy(
        upd_out.at[me_lat], out.at[:, pl.ds(pl.multiple_of(me_lat * cols, cols), cols), :], s4.at[0]
    )
    own.start()
    for copy in sends1:
        copy.wait_send()
    for copy in sends2:
        copy.wait_send()
    lax.fori_loop(1, total, wait_att_send, 0)
    own.wait()
    for copy in sends4:
        copy.wait()


def fused_body(
    fields, norm_lon, query_lon, key_lon, value_lon, out_lon, temp_lon, bias_lon,
    norm_lat, query_lat, key_lat, value_lat, out_lat, temp_lat, bias_lat,
    norm_mlp, w_gate, w_up, w_down,
):
    rows, width, depth = fields.shape
    heads = temp_lon.shape[0]
    n_lon, n_lat = lax.axis_size("lon"), lax.axis_size("lat")
    cols = width // n_lat
    nlon = width * n_lon
    total = n_lon * n_lat
    place = np.arange(nlon)
    wave = np.cos((place[:, None] - place[None, :]) * (2.0 * math.pi / nlon)).astype(np.float32)
    hbm = pl.BlockSpec(memory_space=pl.ANY)
    weights = (query_lon, key_lon, value_lon, out_lon, query_lat, key_lat, value_lat, out_lat,
               w_gate, w_up, w_down)
    dma = pltpu.SemaphoreType.DMA
    updated = pl.pallas_call(
        functools.partial(block_kernel, n_lon, n_lat, rows, width, depth, heads),
        out_shape=pltpu.VMEM((rows, width, depth), BF16),
        in_specs=[hbm] * 20,
        out_specs=hbm,
        scratch_shapes=[pltpu.VMEM((rows, width, depth), BF16)]
        + [pltpu.VMEM((1, depth), F32)] * 3
        + [pltpu.VMEM((1, heads), F32)] * 4
        + [pltpu.VMEM((nlon, nlon), F32)]
        + [pltpu.VMEM(w.shape, w.dtype) for w in weights]
        + [
            pltpu.VMEM((rows, width, depth), BF16),
            pltpu.VMEM((n_lon, width, depth), BF16),
            pltpu.VMEM((n_lat, rows, cols, depth), BF16),
            pltpu.VMEM((n_lat, rows, cols, depth), BF16),
            pltpu.VMEM((total, cols, depth), BF16),
            pltpu.VMEM((n_lat * rows, cols, depth), BF16),
            pltpu.VMEM((n_lat, rows, cols, depth), BF16),
            dma((20,)),
            dma((n_lon,)), dma((n_lon,)),
            dma((n_lat,)), dma((n_lat,)),
            dma((total,)), dma((total,)),
            dma((n_lat,)), dma((n_lat,)),
        ],
        compiler_params=pltpu.CompilerParams(collective_id=0, has_side_effects=True),
    )(
        fields, norm_lon[None], norm_lat[None], norm_mlp[None], temp_lon[None], bias_lon[None],
        temp_lat[None], bias_lat[None],
        jnp.asarray(wave), *weights,
    )
    return updated


def choose(*args):
    rows, width, _ = args[0].shape
    n_lon, n_lat = lax.axis_size("lon"), lax.axis_size("lat")
    if rows == n_lon and width % n_lat == 0 and width // n_lat == 8:
        return fused_body(*args)
    return body(*args)


def solution(mesh):
    in_specs = (P("lat", "lon", None),) + (P(),) * 18
    out_specs = P("lat", "lon", None)
    return jax.shard_map(choose, mesh=mesh, in_specs=in_specs, out_specs=out_specs, check_vma=False)
```

profile of v0, /device:TPU:0, one launch (start us, length us, event | category | flops | bytes accessed | tf_op | source)
XLA Modules:
  0.0 25.8 jit_solution(8919091077955762233)
XLA Ops:
  0.0 25.1 %shard_map.190 = bf16[8,32,256]{2,1,0:T(8,128)(2,1)S(1)} custom-call(bf16[8,32,256]{2,1,0:T(8,128)(2,1)} %fields_h.1, f32[1,256]{1,0:T(1,128)} %bitcast.7, f32[1,256]{1,0:T(1,128)} %bitcast.8, f32[1,256]{1,0:T(1,128)} %bitcast.9, f32[1,8]{1,0:T(1,128)} %bitcast.10, f32[1,8]{1,0:T(1,128)} %bitcast.11, f32[1,8]{1,0:T(1,128)} %bitcast.12, f32[1,8]{1,0:T(1,128)} %bitcast.13, ...), custom_call_target="tpu_custom_call" | custom-call | tf_op jit(solution)/shard_map/pallas_call | solution.py:380
  25.1 0.7 %copy.22 = bf16[8,32,256]{2,1,0:T(8,128)(2,1)} copy(bf16[8,32,256]{2,1,0:T(8,128)(2,1)S(1)} %shard_map.190) | data formatting | bytes 262144
where the time goes:
time: 26.3 us; the launch traced here: 25.8 us
  Pallas kernels  25.1 us (95%)
  local copies, waits for them, and re-layouts  0.66 us (3%)
    pallas_call x1, Pallas kernels, fused_body(): pl.pallas_call(functools.partial(block_kernel, n_lon, n_lat, rows, width,...  25.1 us
    unnamed x1, local copies, waits for them, and re-layouts  0.66 us

commit v1 on v0

v1 whole, which is shorter than its diff:
```python
import math

import jax
import jax.numpy as jnp
import functools
import numpy as np
from jax import lax
from jax.experimental import pallas as pl
from jax.experimental.pallas import tpu as pltpu
from jax.sharding import PartitionSpec as P


def normalize(values, gain):
    factor = lax.rsqrt(jnp.mean(values * values, axis=-1, keepdims=True) + 1e-06)
    return (values * factor * gain).astype(jnp.bfloat16)


def project(values, weight):
    return jnp.dot(values, weight, preferred_element_type=jnp.float32).astype(jnp.bfloat16)


def attend_lat(queries, keys, values, temp, bias):
    count, cols, depth = queries.shape
    heads = temp.shape[0]
    size = depth // heads
    qh = queries.reshape(count, cols, heads, size)
    kh = keys.reshape(count, cols, heads, size)
    vh = values.reshape(count, cols, heads, size)
    scores = jnp.einsum("ichd,jchd->chij", qh, kh, preferred_element_type=jnp.float32)
    place = jnp.arange(count, dtype=jnp.int32)
    spread = jnp.abs(place[:, None] - place[None, :]).astype(jnp.float32) / count
    scores = (
        scores * (temp / math.sqrt(size))[None, :, None, None]
        + bias[None, :, None, None] * spread[None, None]
    )
    expo = jnp.exp(scores - jnp.max(scores, axis=-1, keepdims=True))
    denom = jnp.sum(expo, axis=-1)
    mixed = jnp.einsum(
        "chij,jchd->ichd", expo.astype(jnp.bfloat16), vh, preferred_element_type=jnp.float32
    )
    mixed = mixed / jnp.transpose(denom, (2, 0, 1))[..., None]
    return mixed.astype(jnp.bfloat16).reshape(count, cols, depth)


def body(
    fields,
    norm_lon,
    query_lon,
    key_lon,
    value_lon,
    out_lon,
    temp_lon,
    bias_lon,
    norm_lat,
    query_lat,
    key_lat,
    value_lat,
    out_lat,
    temp_lat,
    bias_lat,
    norm_mlp,
    w_gate,
    w_up,
    w_down,
):
    rows, width, depth = fields.shape
    heads = temp_lon.shape[0]
    size = depth // heads
    total_lon = width * lax.axis_size("lon")
    resid = fields.astype(jnp.float32)
    normed = normalize(resid, norm_lon)
    scale_lon = temp_lon / math.sqrt(size)
    query_place = lax.axis_index("lon") * width + jnp.arange(width, dtype=jnp.int32)
    queries = project(normed, query_lon).reshape(rows, width, heads, size)
    piece = lax.all_gather(normed, "lon", axis=1, tiled=True)
    keys = project(piece, key_lon)
    count = keys.shape[1]
    key_place = jnp.arange(count, dtype=jnp.int32)
    angle = (query_place[:, None] - key_place[None, :]).astype(jnp.float32) * (
        2.0 * math.pi / total_lon
    )
    wave = jnp.cos(angle)

    def one_row(items):
        query_row, key_row, value_row, peak, total, accum = items
        key_heads = key_row.reshape(count, heads, size)
        value_heads = value_row.reshape(count, heads, size)
        scores = jnp.einsum(
            "ihd,jhd->hij", query_row, key_heads, preferred_element_type=jnp.float32
        )
        scores = scores * scale_lon[:, None, None] + bias_lon[:, None, None] * wave[None]
        fresh = jnp.maximum(peak, jnp.max(scores, axis=-1))
        shrink = jnp.exp(peak - fresh)
        expo = jnp.exp(scores - fresh[..., None])
        total = total * shrink + jnp.sum(expo, axis=-1)
        mixed = jnp.einsum(
            "hij,jhd->ihd",
            expo.astype(jnp.bfloat16),
            value_heads,
            preferred_element_type=jnp.float32,
        )
        accum = accum.reshape(width, heads, size) * jnp.transpose(shrink)[:, :, None] + mixed
        return (fresh, total, accum.reshape(width, depth))

    peak = jnp.full((rows, heads, width), -1e30, jnp.float32)
    total = jnp.zeros((rows, heads, width), jnp.float32)
    accum = jnp.zeros((rows, width, depth), jnp.float32)
    peak, total, accum = lax.map(
        one_row, (queries, keys, project(piece, value_lon), peak, total, accum)
    )
    attended = accum.reshape(rows, width, heads, size) / jnp.transpose(total, (0, 2, 1))[..., None]
    attended = attended.astype(jnp.bfloat16).reshape(rows, width, depth)
    first = resid + jnp.dot(attended, out_lon, preferred_element_type=jnp.float32)
    normed_lat = normalize(first, norm_lat)
    query_col = project(normed_lat, query_lat)
    key_col = project(normed_lat, key_lat)
    value_col = project(normed_lat, value_lat)
    query_col, key_col, value_col = (
        lax.all_to_all(query_col, "lat", split_axis=1, concat_axis=0, tiled=True),
        lax.all_to_all(key_col, "lat", split_axis=1, concat_axis=0, tiled=True),
        lax.all_to_all(value_col, "lat", split_axis=1, concat_axis=0, tiled=True),
    )
    mixed_lat = attend_lat(query_col, key_col, value_col, temp_lat, bias_lat)
    returned = lax.all_to_all(mixed_lat, "lat", split_axis=0, concat_axis=1, tiled=True)
    second = first + jnp.dot(returned, out_lat, preferred_element_type=jnp.float32)
    normed_mlp = normalize(second, norm_mlp)
    gate = jnp.dot(normed_mlp, w_gate, preferred_element_type=jnp.float32)
    upper = jnp.dot(normed_mlp, w_up, preferred_element_type=jnp.float32)
    hidden = (jax.nn.silu(gate) * upper).astype(jnp.bfloat16)
    return (second + jnp.dot(hidden, w_down, preferred_element_type=jnp.float32)).astype(
        jnp.bfloat16
    )


NT = (((1,), (1,)), ((), ()))
MESH = pl.DeviceIdType.MESH
F32 = jnp.float32
BF16 = jnp.bfloat16
LANES = 128
LOG2E = math.log2(math.e)


def mm(a, b):
    return jnp.dot(a, b, preferred_element_type=F32)


def mm_nt(a, b):
    return lax.dot_general(a, b, NT, preferred_element_type=F32)


def iota(shape, dim):
    return lax.broadcasted_iota(jnp.int32, shape, dim)


def partner(me, step, n):
    if n & (n - 1):
        return lax.rem(me + step, n)
    bits = [b for b in range(n.bit_length()) if step >> b & 1]
    return sum((1 - 2 * lax.rem(me // (1 << b), 2)) * (1 << b) for b in bits) + me


def far_first(n):
    return sorted(range(1, n), key=lambda step: -(2 * (step >> 1).bit_count() + (step & 1)))


def split_pairs(values, odd):
    high = values.astype(BF16).astype(F32)
    return jnp.where(odd, values - high, high)


class Attention:
    def __init__(self, keys, extra_keys, queries_t, extras, values_t, size):
        self.keys, self.extra_keys, self.queries_t, self.extras = keys, extra_keys, queries_t, extras
        self.values_t, self.size = values_t, size
        self.stages = (self.scores, self.weights, self.mixed, self.divided)
        self.held = {}

    def scores(self, b, h):
        size = self.size
        per_group = LANES // size
        group = h // per_group
        blank = jnp.zeros((size, LANES), BF16)
        pieces = []
        for g in range(group * per_group, (group + 1) * per_group):
            rows = self.queries_t[g * size:(g + 1) * size, b * LANES:(b + 1) * LANES]
            pieces.append(jnp.concatenate([rows if g == h else blank, rows if g == h + 1 else blank], axis=1))
        pieces.append(jnp.concatenate([self.extras(b, h), self.extras(b, h + 1)], axis=1))
        left = jnp.concatenate([self.keys[:, group * LANES:(group + 1) * LANES], self.extra_keys], axis=1)
        self.held[b, h] = mm(left, jnp.concatenate(pieces, axis=0))

    def weights(self, b, h):
        scores = self.held[b, h]
        self.held[b, h] = jnp.exp2((scores - jnp.max(scores, axis=0, keepdims=True)).astype(BF16))

    def mixed(self, b, h):
        ones = jnp.ones((16, self.keys.shape[0]), BF16)
        left = jnp.concatenate([self.values_t[h * self.size:(h + 2) * self.size, :], ones], axis=0)
        self.held[b, h] = mm(left, self.held[b, h])

    def divided(self, b, h):
        size = self.size
        mixed = self.held[b, h]
        share = 1.0 / mixed[2 * size:2 * size + 1, :]
        self.held[b, h] = jnp.concatenate(
            [mixed[:size, :LANES] * share[:, :LANES], mixed[size:2 * size, LANES:] * share[:, LANES:]], axis=0
        )

    def taken(self, b, heads):
        return jnp.concatenate([self.held.pop((b, h)) for h in range(0, heads, 2)], axis=0).T


def staggered(stages, units, after):
    for step in range(len(units) + len(stages) - 1):
        for s, stage in enumerate(stages):
            if 0 <= step - s < len(units):
                stage(*units[step - s])
        if step >= len(stages) - 1:
            after(*units[step - len(stages) + 1])


def block_kernel(
    n_lon, n_lat, rows, width, depth, heads,
    fields_h, gain_lon_h, gain_lat_h, gain_mlp_h, temp_lon_h, bias_lon_h, temp_lat_h, bias_lat_h,
    ktab_h, qtab_h, wq1_h, wk1_h, wv1_h, wo1_h, wq2_h, wk2_h, wv2_h, wo2_h, wg_h, wu_h, wd_h,
    out,
    fields, gain_lon, gain_lat, gain_mlp, temp_lon, bias_lon, temp_lat, bias_lat,
    ktab, qtab, wq1, wk1, wv1, wo1, wq2, wk2, wv2, wo2, wg, wu, wd,
    norm_out, norm_in, field_out, field_in, att_out, att_in, upd_out,
    wqv1, wqv2, extra1, extra2, onehot,
    local_sem, s1, r1, s2, r2, s3, r3, s4, r4, line_sem, plane_sem,
):
    me_lon = lax.axis_index("lon")
    me_lat = lax.axis_index("lat")
    total = n_lon * n_lat
    size = depth // heads
    cols = width // n_lat
    count = n_lat * rows
    cells = rows * width
    half = n_lat // 2
    side = me_lat // half
    own = lax.rem(me_lat, half)
    far = (1 - side) * half

    def lat_at(slot):
        return lax.rem(slot + far, n_lat)

    loads = {}

    def load(name, src, dst):
        loads[name] = pltpu.make_async_copy(src, dst, local_sem.at[len(loads)])
        loads[name].start()

    load("fields", fields_h, fields)
    load("gain_lon", gain_lon_h, gain_lon)
    barrier = pltpu.get_barrier_semaphore()
    order = far_first(n_lon)

    def signal_plane(sem):
        for step in order:
            pl.semaphore_signal(
                sem, inc=1, device_id=(partner(me_lon, step, n_lon), me_lat), device_id_type=MESH
            )

    def signal_line(sem):
        @pl.when(me_lat > 0)
        def _():
            pl.semaphore_signal(sem, inc=1, device_id=(me_lon, me_lat - 1), device_id_type=MESH)

        @pl.when(me_lat < n_lat - 1)
        def _():
            pl.semaphore_signal(sem, inc=1, device_id=(me_lon, me_lat + 1), device_id_type=MESH)

    beside = jnp.minimum(me_lat, 1) + jnp.minimum(n_lat - 1 - me_lat, 1)
    signal_plane(barrier)
    signal_line(barrier)
    load("ktab0", ktab_h.at[pl.ds(far, half)], ktab.at[pl.ds(0, half)])
    load("ktab1", ktab_h.at[pl.ds(half - far, half)], ktab.at[pl.ds(half, half)])
    load("qtab0", qtab_h.at[pl.ds(1 - side, 1)], qtab.at[pl.ds(0, 1)])
    load("qtab1", qtab_h.at[pl.ds(side, 1)], qtab.at[pl.ds(1, 1)])
    for name, src, dst in [
        ("wq1", wq1_h, wq1), ("wk1", wk1_h, wk1), ("wv1", wv1_h, wv1), ("temp_lon", temp_lon_h, temp_lon),
        ("bias_lon", bias_lon_h, bias_lon), ("temp_lat", temp_lat_h, temp_lat), ("bias_lat", bias_lat_h, bias_lat),
        ("wo1", wo1_h, wo1), ("wq2", wq2_h, wq2), ("wk2", wk2_h, wk2), ("wv2", wv2_h, wv2), ("wo2", wo2_h, wo2),
        ("wg", wg_h, wg), ("wu", wu_h, wu), ("wd", wd_h, wd), ("gain_lat", gain_lat_h, gain_lat),
        ("gain_mlp", gain_mlp_h, gain_mlp),
    ]:
        load(name, src, dst)

    loads["fields"].wait()
    loads["gain_lon"].wait()
    wide = fields[...].astype(F32)
    factor = lax.rsqrt(jnp.mean(wide * wide, axis=-1, keepdims=True) + 1e-06)
    scaled = (wide * factor * gain_lon[...][None]).reshape(rows, n_lat, cols, depth).astype(BF16)
    pieces = wide.reshape(rows, n_lat, cols, depth).astype(BF16)
    for a in range(n_lat):
        norm_out[:, pl.ds(lax.rem(a + n_lat - far, n_lat), 1)] = scaled[:, a:a + 1]
        field_out[a] = pieces[:, a]

    pl.semaphore_wait(barrier, n_lon - 1 + beside)

    def my_cols(ref):
        return ref.at[:, pl.ds(pl.multiple_of(me_lat * cols, cols), cols), :]

    def send_norm(step):
        peer = partner(me_lon, step, n_lon)
        return pltpu.make_async_remote_copy(
            src_ref=norm_out.at[peer], dst_ref=norm_in.at[:, me_lon],
            send_sem=s1.at[0], recv_sem=r1.at[0], device_id=(peer, me_lat), device_id_type=MESH,
        )

    def send_field(peer):
        slot = lax.rem(me_lat + n_lat - (1 - peer // half) * half, n_lat)
        return pltpu.make_async_remote_copy(
            src_ref=field_out.at[peer], dst_ref=field_in.at[slot], send_sem=s2.at[0],
            recv_sem=r2.at[0], device_id=(me_lon, peer), device_id_type=MESH,
        )

    def send_fields(hop):
        @pl.when(me_lat >= hop)
        def _():
            send_field(me_lat - hop).start()

        @pl.when(me_lat + hop < n_lat)
        def _():
            send_field(me_lat + hop).start()

    def whole(src, dst, sends, recvs):
        return pltpu.make_async_remote_copy(
            src_ref=src, dst_ref=dst, send_sem=sends, recv_sem=recvs,
            device_id=(me_lon, me_lat), device_id_type=MESH,
        )

    for step in order:
        send_norm(step).start()
    for hop in range(1, n_lat):
        if hop > 1:
            pl.semaphore_wait(line_sem.at[hop - 1], beside)
        if hop < n_lat - 1:
            signal_line(line_sem.at[hop])
        send_fields(hop)
    signal_plane(plane_sem)
    norm_in[:, pl.ds(me_lon, 1)] = norm_out[pl.ds(me_lon, 1)].reshape(n_lat, 1, cols, depth)
    field_in[pl.ds(half + own, 1)] = field_out[pl.ds(me_lat, 1)]

    for name in ("wq1", "wk1", "wv1", "temp_lon", "bias_lon", "temp_lat", "bias_lat", "ktab0", "ktab1", "qtab0", "qtab1"):
        loads[name].wait()
    wqv1[:depth] = wq1[...].T
    wqv1[depth:] = wv1[...].T
    shape = (16, LANES)
    odd = lax.rem(iota(shape, 0), 2) == 1
    for h in range(heads):
        for b in range(2):
            extra1[b, h] = split_pairs(bias_lon[:, h:h + 1] * LOG2E * qtab[b], odd).astype(BF16)
    lanes = iota((cells, LANES), 1)
    slot = iota((cells, LANES), 0) // cols
    col = lax.rem(iota((cells, LANES), 0), cols)
    hot = (lanes == slot) | (lanes == slot + count) | (lanes == col + 2 * count)
    onehot[...] = jnp.where(hot, 1.0, 0.0).astype(BF16)
    shape = (LANES, LANES)
    line = iota(shape, 0)
    for b in range(2):
        cell = iota(shape, 1) + b * LANES
        here = lax.rem(line + far * rows, count)
        there = lax.rem(cell // cols + far * rows, count)
        apart = jnp.abs(here - there).astype(F32) / count
        fence = jnp.where(line - 2 * count == lax.rem(cell, cols), 0.0, -1e30)
        for h in range(heads):
            term = split_pairs(bias_lat[:, h:h + 1] * LOG2E * apart, line >= count)
            term = jnp.where(line < 2 * count, term, jnp.where(line < 2 * count + cols, fence, 0.0))
            extra2[b, h] = term.astype(BF16)

    def scales(temp):
        return [jnp.broadcast_to(temp[:, h:h + 1] * (LOG2E / math.sqrt(size)), (size, LANES)) for h in range(heads)]

    def scaled_t(queries_t, temp):
        factors = [jnp.concatenate([one] * (queries_t.shape[1] // LANES), axis=1) for one in temp]
        return (queries_t * jnp.concatenate(factors, axis=0)).astype(BF16)

    scale_lon = scales(temp_lon)
    norm_all = whole(norm_out.at[pl.ds(0, n_lon - 1)], norm_out.at[pl.ds(0, n_lon - 1)], s1.at[0], r1.at[0])
    norm_all.wait_recv()

    nlon = n_lon * width
    normed = norm_in[...].reshape(nlon, depth)
    keys = mm(normed, wk1[...]).astype(BF16)
    both_t = mm_nt(wqv1[...], normed)
    queries_t = scaled_t(both_t[:depth], scale_lon)
    values_t = both_t[depth:].astype(BF16)
    key_extra = ktab[...].reshape(nlon, LANES)
    pad = jnp.zeros((LANES - 16, LANES), BF16)

    def send_att(slot, peer, group):
        index = slot * n_lon + peer
        return pltpu.make_async_remote_copy(
            src_ref=att_out.at[index], dst_ref=att_in.at[group * rows + me_lon], send_sem=s3.at[0],
            recv_sem=r3.at[group // half], device_id=(peer, lat_at(slot)), device_id_type=MESH,
        )

    units = [(b, h) for b in range(2) for h in range(0, heads, 2)]
    row_work = Attention(
        keys, key_extra, queries_t, lambda b, h: jnp.concatenate([extra1[b, h], pad], axis=0), values_t, size
    )

    def row_done(b, h):
        if h < heads - 2:
            return
        att = row_work.taken(b, heads)
        att_out[b * half * n_lon:(b + 1) * half * n_lon] = att.reshape(half * n_lon, cols, depth).astype(BF16)
        if b == 0:
            pl.semaphore_wait(plane_sem, n_lon - 1)
            for step in range(half):
                slot = step + (1 - side) * (half - 1 - 2 * step)
                for hop in order + [0]:
                    send_att(slot, partner(me_lon, hop, n_lon), own).start()
        else:
            for step in list(range(1, half)) + [0]:
                for hop in order + [0]:
                    if step or hop:
                        slot = half + lax.rem(own + step, half)
                        send_att(slot, partner(me_lon, hop, n_lon), half + own).start()

    staggered(row_work.stages, units, row_done)
    my_slot = (half + own) * rows + me_lon
    att_in[pl.ds(my_slot, 1)] = att_out[pl.ds((half + own) * n_lon + me_lon, 1)]

    for name in ("wo1", "wq2", "wk2", "wv2", "wo2", "wg", "wu", "wd", "gain_lat", "gain_mlp"):
        loads[name].wait()
    wqv2[:depth] = wq2[...].T
    wqv2[depth:] = wv2[...].T
    scale_lat = scales(temp_lat)
    field_all = whole(field_out.at[pl.ds(0, n_lat - 1)], field_in.at[pl.ds(0, n_lat - 1)], s2.at[0], r2.at[0])
    field_all.wait_recv()

    near_all = whole(att_out.at[pl.ds(0, count // 2 - 1)], att_in.at[pl.ds(0, count // 2 - 1)], s3.at[0], r3.at[1])
    far_all = whole(att_out.at[pl.ds(0, count // 2)], att_in.at[pl.ds(0, count // 2)], s3.at[0], r3.at[0])
    att_all = whole(att_out.at[pl.ds(0, total - 1)], att_in.at[pl.ds(0, total - 1)], s3.at[0], r3.at[0])
    near_all.wait_recv()
    far_all.wait_recv()

    resid = field_in[...].astype(F32).reshape(cells, depth)
    attended = att_in[...].astype(F32).reshape(cells, depth).astype(BF16)
    first = resid + mm(attended, wo1[...])
    normed = normalize(first, gain_lat[...])
    keys = mm(normed, wk2[...]).astype(BF16)
    both_t = mm_nt(wqv2[...], normed)
    queries_t = scaled_t(both_t[:depth], scale_lat)
    values_t = both_t[depth:].astype(BF16)
    ff = wg.shape[1]
    step_ff = min(ff, 256)

    def send_upd(slot):
        return pltpu.make_async_remote_copy(
            src_ref=upd_out.at[slot], dst_ref=my_cols(out), send_sem=s4.at[0], recv_sem=r4.at[0],
            device_id=(me_lon, lat_at(slot)), device_id_type=MESH,
        )

    col_work = Attention(keys, onehot[...], queries_t, lambda b, h: extra2[b, h], values_t, size)

    def col_done(b, h):
        if h < heads - 2:
            return
        second = first[b * LANES:(b + 1) * LANES] + mm(col_work.taken(b, heads).astype(BF16), wo2[...])
        normed = normalize(second, gain_mlp[...])
        for f in range(0, ff, step_ff):
            gate = mm(normed, wg[:, f:f + step_ff])
            upper = mm(normed, wu[:, f:f + step_ff])
            hidden = (gate * (0.5 * jnp.tanh(0.5 * gate) + 0.5) * upper).astype(BF16)
            second = second + mm(hidden, wd[f:f + step_ff, :])
        upd_out[b * half:(b + 1) * half] = second.reshape(half, rows, cols, depth).astype(BF16)
        if b == 0:
            new = [send_upd(step + (1 - side) * (half - 1 - 2 * step)) for step in range(half)]
        else:
            new = [send_upd(half + lax.rem(own + step, half)) for step in range(1, half)]
        for copy in new:
            copy.start()

    staggered(col_work.stages, units, col_done)
    mine = pltpu.make_async_copy(upd_out.at[half + own], my_cols(out), s4.at[1])
    mine.start()
    norm_all.wait_send()
    field_all.wait_send()
    att_all.wait_send()
    mine.wait()
    upd_all = whole(upd_out.at[pl.ds(0, n_lat - 1)], upd_out.at[pl.ds(0, n_lat - 1)], s4.at[0], r4.at[0])
    upd_all.wait_send()
    upd_all.wait_recv()


def fused_body(
    fields, norm_lon, query_lon, key_lon, value_lon, out_lon, temp_lon, bias_lon,
    norm_lat, query_lat, key_lat, value_lat, out_lat, temp_lat, bias_lat,
    norm_mlp, w_gate, w_up, w_down,
):
    rows, width, depth = fields.shape
    heads = temp_lon.shape[0]
    n_lon, n_lat = lax.axis_size("lon"), lax.axis_size("lat")
    cols = width // n_lat
    nlon = width * n_lon
    total = n_lon * n_lat
    cells = rows * width
    place = np.arange(nlon).reshape(n_lon, n_lat, cols).transpose(1, 0, 2).reshape(nlon)
    turn = place * (2.0 * math.pi / nlon)
    waves = np.stack([np.cos(turn)] * 4 + [np.sin(turn)] * 4, axis=1).astype(np.float32)
    high = waves.astype(jnp.bfloat16).astype(np.float32)
    ktab = np.zeros((nlon, LANES), np.float32)
    ktab[:, :8] = np.where(np.arange(8)[None] % 4 < 2, high, waves - high)
    ktab = ktab.astype(jnp.bfloat16).reshape(n_lat, n_lon * cols, LANES)
    qtab = np.zeros((2, 16, LANES), np.float32)
    qtab[:, :8] = waves.reshape(2, LANES, 8).transpose(0, 2, 1)
    hbm = pl.BlockSpec(memory_space=pl.ANY)
    weights = (query_lon, key_lon, value_lon, out_lon, query_lat, key_lat, value_lat, out_lat,
               w_gate, w_up, w_down)
    dma = pltpu.SemaphoreType.DMA
    updated = pl.pallas_call(
        functools.partial(block_kernel, n_lon, n_lat, rows, width, depth, heads),
        out_shape=pltpu.VMEM((rows, width, depth), BF16),
        in_specs=[hbm] * 21,
        out_specs=hbm,
        scratch_shapes=[pltpu.VMEM((rows, width, depth), BF16)]
        + [pltpu.VMEM((1, depth), F32)] * 3
        + [pltpu.VMEM((1, heads), F32)] * 4
        + [pltpu.VMEM(ktab.shape, BF16), pltpu.VMEM(qtab.shape, F32)]
        + [pltpu.VMEM(w.shape, w.dtype) for w in weights]
        + [
            pltpu.VMEM((rows, n_lat, cols, depth), BF16),
            pltpu.VMEM((n_lat, n_lon, cols, depth), BF16),
            pltpu.VMEM((n_lat, rows, cols, depth), BF16),
            pltpu.VMEM((n_lat, rows, cols, depth), BF16),
            pltpu.VMEM((total, cols, depth), BF16),
            pltpu.VMEM((n_lat * rows, cols, depth), BF16),
            pltpu.VMEM((n_lat, rows, cols, depth), BF16),
            pltpu.VMEM((2 * depth, depth), BF16),
            pltpu.VMEM((2 * depth, depth), BF16),
            pltpu.VMEM((2, heads, 16, LANES), BF16),
            pltpu.VMEM((2, heads, LANES, LANES), BF16),
            pltpu.VMEM((cells, LANES), BF16),
            dma((24,)),
            dma((1,)), dma((1,)),
            dma((1,)), dma((1,)),
            dma((1,)), dma((2,)),
            dma((2,)), dma((1,)),
            pltpu.SemaphoreType.REGULAR((n_lat,)),
            pltpu.SemaphoreType.REGULAR,
        ],
        compiler_params=pltpu.CompilerParams(collective_id=0, has_side_effects=True),
    )(
        fields, norm_lon[None], norm_lat[None], norm_mlp[None], temp_lon[None], bias_lon[None],
        temp_lat[None], bias_lat[None],
        jnp.asarray(ktab), jnp.asarray(qtab), *weights,
    )
    return updated


def fits(rows, width, n_lon, n_lat, heads, depth):
    return (
        rows == n_lon and n_lat % 2 == 0 and width == 8 * n_lat and rows * width == 2 * LANES
        and width * n_lon == 2 * LANES and 2 * n_lat * rows + width // n_lat <= LANES
        and LANES % (depth // heads) == 0 and LANES // (depth // heads) % 2 == 0
    )


def choose(*args):
    rows, width, _ = args[0].shape
    n_lon, n_lat = lax.axis_size("lon"), lax.axis_size("lat")
    if fits(rows, width, n_lon, n_lat, args[6].shape[0], args[0].shape[2]):
        return fused_body(*args)
    return body(*args)


def solution(mesh):
    in_specs = (P("lat", "lon", None),) + (P(),) * 18
    out_specs = P("lat", "lon", None)
    return jax.shard_map(choose, mesh=mesh, in_specs=in_specs, out_specs=out_specs, check_vma=False)
```

time: 26.3 us -> 22.5 us (0.86); the launches traced: 25.8 us -> 22.4 us
  Pallas kernels: 25.1 us -> 21.7 us
    pallas_call x1, Pallas kernels: 25.1 us -> 21.7 us  [fused_body(): pl.pallas_call(functools.partial(block_kernel, n_lon, n_lat, rows, width,...]
where the time goes in v1:
time: 22.5 us; the launch traced here: 22.4 us
  Pallas kernels  21.7 us (96%)
  local copies, waits for them, and re-layouts  0.66 us (3%)
    pallas_call x1, Pallas kernels, fused_body(): pl.pallas_call(functools.partial(block_kernel, n_lon, n_lat, rows, width,...  21.7 us
    unnamed x1, local copies, waits for them, and re-layouts  0.66 us

profile of v1, /device:TPU:0, one launch (start us, length us, event | category | flops | bytes accessed | tf_op | source)
XLA Modules:
  0.0 22.4 jit_solution(8394111278467468158)
XLA Ops:
  0.0 21.7 %shard_map.199 = bf16[8,32,256]{2,1,0:T(8,128)(2,1)S(1)} custom-call(bf16[8,32,256]{2,1,0:T(8,128)(2,1)} %fields_h.1, f32[1,256]{1,0:T(1,128)} %bitcast.7, f32[1,256]{1,0:T(1,128)} %bitcast.8, f32[1,256]{1,0:T(1,128)} %bitcast.9, f32[1,8]{1,0:T(1,128)} %bitcast.10, f32[1,8]{1,0:T(1,128)} %bitcast.11, f32[1,8]{1,0:T(1,128)} %bitcast.12, f32[1,8]{1,0:T(1,128)} %bitcast.13, ...), custom_call_target="tpu_custom_call" | custom-call | tf_op jit(solution)/shard_map/pallas_call | solution.py:514
  21.7 0.7 %copy.23 = bf16[8,32,256]{2,1,0:T(8,128)(2,1)} copy(bf16[8,32,256]{2,1,0:T(8,128)(2,1)S(1)} %shard_map.199) | data formatting | bytes 262144

commit v2 on v1

--- a/solution.py
+++ b/solution.py
@@ -168,45 +168,86 @@
     return jnp.where(odd, values - high, high)
 
 
-class Attention:
-    def __init__(self, keys, extra_keys, queries_t, extras, values_t, size):
-        self.keys, self.extra_keys, self.queries_t, self.extras = keys, extra_keys, queries_t, extras
-        self.values_t, self.size = values_t, size
-        self.stages = (self.scores, self.weights, self.mixed, self.divided)
+class Quads:
+    def __init__(self, left, right, table, values, size):
+        self.left, self.right, self.table, self.values, self.size = left, right, table, values, size
+        self.stages = (self.scores, self.weights, self.mixed, self.turned)
         self.held = {}
 
-    def scores(self, b, h):
-        size = self.size
-        per_group = LANES // size
-        group = h // per_group
-        blank = jnp.zeros((size, LANES), BF16)
-        pieces = []
-        for g in range(group * per_group, (group + 1) * per_group):
-            rows = self.queries_t[g * size:(g + 1) * size, b * LANES:(b + 1) * LANES]
-            pieces.append(jnp.concatenate([rows if g == h else blank, rows if g == h + 1 else blank], axis=1))
-        pieces.append(jnp.concatenate([self.extras(b, h), self.extras(b, h + 1)], axis=1))
-        left = jnp.concatenate([self.keys[:, group * LANES:(group + 1) * LANES], self.extra_keys], axis=1)
-        self.held[b, h] = mm(left, jnp.concatenate(pieces, axis=0))
-
-    def weights(self, b, h):
-        scores = self.held[b, h]
-        self.held[b, h] = jnp.exp2((scores - jnp.max(scores, axis=0, keepdims=True)).astype(BF16))
-
-    def mixed(self, b, h):
-        ones = jnp.ones((16, self.keys.shape[0]), BF16)
-        left = jnp.concatenate([self.values_t[h * self.size:(h + 2) * self.size, :], ones], axis=0)
-        self.held[b, h] = mm(left, self.held[b, h])
-
-    def divided(self, b, h):
-        size = self.size
+    def scores(self, *unit):
+        scores = mm(self.left(*unit), self.right(*unit))
+        if self.table is not None:
+            scores = scores + self.table(*unit)
+        self.held[unit] = scores
+
+    def weights(self, *unit):
+        scores = self.held[unit]
+        self.held[unit] = jnp.exp2((scores - jnp.max(scores, axis=0, keepdims=True)).astype(BF16))
+
+    def mixed(self, *unit):
+        self.held[unit] = mm(self.values(*unit), self.held[unit])
+
+    def turned(self, *unit):
+        mixed = self.held[unit]
+        share = 1.0 / mixed[LANES:LANES + 1, :]
+        parts = []
+        for i in range(LANES // self.size):
+            lane = slice(i // 2 * LANES, (i // 2 + 1) * LANES)
+            parts.append(mixed[i * self.size:(i + 1) * self.size, lane] * share[:, lane])
+        both = jnp.concatenate(parts, axis=0).T
+        odd = lax.rem(iota((LANES // 2, LANES), 1) // self.size, 2) == 1
+        self.held[unit] = jnp.where(odd, both[LANES // 2:], both[:LANES // 2])
+
+
+class Pairs(Quads):
+    def turned(self, b, h):
         mixed = self.held[b, h]
-        share = 1.0 / mixed[2 * size:2 * size + 1, :]
+        share = 1.0 / mixed[2 * self.size:2 * self.size + 1, :]
         self.held[b, h] = jnp.concatenate(
-            [mixed[:size, :LANES] * share[:, :LANES], mixed[size:2 * size, LANES:] * share[:, LANES:]], axis=0
-        )
-
-    def taken(self, b, heads):
-        return jnp.concatenate([self.held.pop((b, h)) for h in range(0, heads, 2)], axis=0).T
+            [mixed[:self.size, :LANES] * share[:, :LANES], mixed[self.size:2 * self.size, LANES:] * share[:, LANES:]],
+            axis=0,
+        )
+        if h % 4 == 2:
+            self.held[b, h] = jnp.concatenate([self.held.pop((b, h - 2)), self.held[b, h]], axis=0).T
+
+
+def pair_of(queries_t, h, size):
+    group = h // (LANES // size)
+    blank = jnp.zeros((size, LANES), BF16)
+    pieces = []
+    for g in range(group * (LANES // size), (group + 1) * (LANES // size)):
+        rows = queries_t[g * size:(g + 1) * size]
+        pieces.append(jnp.concatenate([rows if g == h else blank, rows if g == h + 1 else blank], axis=1))
+    return jnp.concatenate(pieces, axis=0)
+
+
+def side_by_side(natural, turned, parity, group, size):
+    lanes = iota((size, LANES), 1)
+    keep = [(lanes < LANES // 2).astype(F32).astype(BF16), (lanes >= LANES // 2).astype(F32).astype(BF16)]
+    blank = jnp.zeros((size, LANES), BF16)
+    pieces = []
+    for i in range(LANES // size):
+        h = group * (LANES // size) + i
+        rows = (natural if i % 2 == parity else turned)[h * size:(h + 1) * size] * keep[i % 2]
+        pieces.append(jnp.concatenate([rows, blank] if i < 2 else [blank, rows], axis=1))
+    return jnp.concatenate(pieces, axis=0)
+
+
+def per_head(values, group, shape):
+    lanes = iota(shape, 1) // (LANES // 2)
+    out = jnp.broadcast_to(values[:, 4 * group:4 * group + 1], shape)
+    for i in range(1, 4):
+        out = jnp.where(lanes == i, values[:, 4 * group + i:4 * group + i + 1], out)
+    return out
+
+
+def root_mean(values):
+    return lax.rsqrt(jnp.mean(values * values, axis=-1, keepdims=True) + 1e-06)
+
+
+def halves_turned(rows):
+    half = LANES // 2
+    return jnp.concatenate([rows[(i ^ 1) * half:((i ^ 1) + 1) * half] for i in range(rows.shape[0] // half)], axis=0)
 
 
 def staggered(stages, units, after):
@@ -226,7 +267,7 @@
     fields, gain_lon, gain_lat, gain_mlp, temp_lon, bias_lon, temp_lat, bias_lat,
     ktab, qtab, wq1, wk1, wv1, wo1, wq2, wk2, wv2, wo2, wg, wu, wd,
     norm_out, norm_in, field_out, field_in, att_out, att_in, upd_out,
-    wqv1, wqv2, extra1, extra2, onehot,
+    wqv1, wqv2, extra1, tables, resid, shuffle, hidden,
     local_sem, s1, r1, s2, r2, s3, r3, s4, r4, line_sem, plane_sem,
 ):
     me_lon = lax.axis_index("lon")
@@ -237,12 +278,21 @@
     count = n_lat * rows
     cells = rows * width
     half = n_lat // 2
+    block = half * rows
     side = me_lat // half
     own = lax.rem(me_lat, half)
-    far = (1 - side) * half
 
     def lat_at(slot):
-        return lax.rem(slot + far, n_lat)
+        if slot < half:
+            return side * slot + (1 - side) * (n_lat - 1 - slot)
+        return side * half + lax.rem(own + 1 + slot - half, half)
+
+    def slot_of(lat, viewer):
+        upper, seen = lat // half, viewer // half
+        distant = upper + seen - 2 * upper * seen
+        far_slot = upper * (n_lat - 1 - lat) + (1 - upper) * lat
+        near_slot = half + lax.rem(lat + 2 * half - 1 - viewer + 2 * half * n_lat, half)
+        return distant * far_slot + (1 - distant) * near_slot
 
     loads = {}
 
@@ -273,10 +323,9 @@
     beside = jnp.minimum(me_lat, 1) + jnp.minimum(n_lat - 1 - me_lat, 1)
     signal_plane(barrier)
     signal_line(barrier)
-    load("ktab0", ktab_h.at[pl.ds(far, half)], ktab.at[pl.ds(0, half)])
-    load("ktab1", ktab_h.at[pl.ds(half - far, half)], ktab.at[pl.ds(half, half)])
-    load("qtab0", qtab_h.at[pl.ds(1 - side, 1)], qtab.at[pl.ds(0, 1)])
-    load("qtab1", qtab_h.at[pl.ds(side, 1)], qtab.at[pl.ds(1, 1)])
+    for slot in range(n_lat):
+        load(f"ktab{slot}", ktab_h.at[lat_at(slot)], ktab.at[slot])
+        load(f"qtab{slot}", qtab_h.at[lat_at(slot)], qtab.at[slot])
     for name, src, dst in [
         ("wq1", wq1_h, wq1), ("wk1", wk1_h, wk1), ("wv1", wv1_h, wv1), ("temp_lon", temp_lon_h, temp_lon),
         ("bias_lon", bias_lon_h, bias_lon), ("temp_lat", temp_lat_h, temp_lat), ("bias_lat", bias_lat_h, bias_lat),
@@ -293,7 +342,7 @@
     scaled = (wide * factor * gain_lon[...][None]).reshape(rows, n_lat, cols, depth).astype(BF16)
     pieces = wide.reshape(rows, n_lat, cols, depth).astype(BF16)
     for a in range(n_lat):
-        norm_out[:, pl.ds(lax.rem(a + n_lat - far, n_lat), 1)] = scaled[:, a:a + 1]
+        norm_out[:, pl.ds(slot_of(a, me_lat), 1)] = scaled[:, a:a + 1]
         field_out[a] = pieces[:, a]
 
     pl.semaphore_wait(barrier, n_lon - 1 + beside)
@@ -309,7 +358,7 @@
         )
 
     def send_field(peer):
-        slot = lax.rem(me_lat + n_lat - (1 - peer // half) * half, n_lat)
+        slot = slot_of(me_lat, peer)
         return pltpu.make_async_remote_copy(
             src_ref=field_out.at[peer], dst_ref=field_in.at[slot], send_sem=s2.at[0],
             recv_sem=r2.at[0], device_id=(me_lon, peer), device_id_type=MESH,
@@ -340,34 +389,47 @@
         send_fields(hop)
     signal_plane(plane_sem)
     norm_in[:, pl.ds(me_lon, 1)] = norm_out[pl.ds(me_lon, 1)].reshape(n_lat, 1, cols, depth)
-    field_in[pl.ds(half + own, 1)] = field_out[pl.ds(me_lat, 1)]
-
-    for name in ("wq1", "wk1", "wv1", "temp_lon", "bias_lon", "temp_lat", "bias_lat", "ktab0", "ktab1", "qtab0", "qtab1"):
+    field_in[n_lat - 1:] = field_out[pl.ds(me_lat, 1)]
+
+    for name in ["wq1", "wk1", "wv1", "temp_lon", "bias_lon", "temp_lat", "bias_lat"] + [
+        f"{kind}{slot}" for slot in range(n_lat) for kind in ("ktab", "qtab")
+    ]:
         loads[name].wait()
     wqv1[:depth] = wq1[...].T
     wqv1[depth:] = wv1[...].T
-    shape = (16, LANES)
+    groups = depth // LANES
+    shape = (16, 2 * LANES)
     odd = lax.rem(iota(shape, 0), 2) == 1
-    for h in range(heads):
-        for b in range(2):
-            extra1[b, h] = split_pairs(bias_lon[:, h:h + 1] * LOG2E * qtab[b], odd).astype(BF16)
-    lanes = iota((cells, LANES), 1)
-    slot = iota((cells, LANES), 0) // cols
-    col = lax.rem(iota((cells, LANES), 0), cols)
-    hot = (lanes == slot) | (lanes == slot + count) | (lanes == col + 2 * count)
-    onehot[...] = jnp.where(hot, 1.0, 0.0).astype(BF16)
-    shape = (LANES, LANES)
-    line = iota(shape, 0)
+    halves = iota((16, LANES), 1) < LANES // 2
     for b in range(2):
-        cell = iota(shape, 1) + b * LANES
-        here = lax.rem(line + far * rows, count)
-        there = lax.rem(cell // cols + far * rows, count)
-        apart = jnp.abs(here - there).astype(F32) / count
-        fence = jnp.where(line - 2 * count == lax.rem(cell, cols), 0.0, -1e30)
-        for h in range(heads):
-            term = split_pairs(bias_lat[:, h:h + 1] * LOG2E * apart, line >= count)
-            term = jnp.where(line < 2 * count, term, jnp.where(line < 2 * count + cols, fence, 0.0))
-            extra2[b, h] = term.astype(BF16)
+        wave = jnp.where(halves, qtab[2 * b], qtab[2 * b + 1])
+        wave = jnp.concatenate([wave, wave], axis=1)
+        for h in range(0, heads, 2):
+            weight = jnp.where(
+                iota(shape, 1) < LANES, bias_lon[:, h:h + 1], bias_lon[:, h + 1:h + 2]
+            ) * LOG2E
+            extra1[b, h // 2] = split_pairs(weight * wave, odd).astype(BF16)
+    hold = half * rows
+    shape = (LANES, 2 * LANES)
+    key_cell, query_cell = iota(shape, 0), lax.rem(iota(shape, 1), LANES // 2)
+
+    def lat_value(spot, distant):
+        group = spot // rows
+        value = jnp.zeros(shape, jnp.int32)
+        for g in range(half):
+            value = jnp.where(group == g, lat_at(g if distant else half + g), value)
+        return value * rows + lax.rem(spot, rows)
+
+    key_far, key_near = lat_value(lax.rem(key_cell, hold), True), lat_value(lax.rem(key_cell, hold), False)
+    same = lax.rem(key_cell, LANES // 2) // hold == query_cell // hold
+    for g in range(groups):
+        weight = per_head(bias_lat, g, shape) * (LOG2E / count)
+        for f in range(2):
+            there = lat_value(lax.rem(query_cell, hold), f == 0)
+            for c in range(2):
+                first_part = key_cell < LANES // 2
+                here = jnp.where(first_part, key_far, key_near) if c == 0 else jnp.where(first_part, key_near, key_far)
+                tables[f, c, g] = jnp.where(same, weight * jnp.abs(here - there).astype(F32), -1e30)
 
     def scales(temp):
         return [jnp.broadcast_to(temp[:, h:h + 1] * (LOG2E / math.sqrt(size)), (size, LANES)) for h in range(heads)]
@@ -386,42 +448,42 @@
     both_t = mm_nt(wqv1[...], normed)
     queries_t = scaled_t(both_t[:depth], scale_lon)
     values_t = both_t[depth:].astype(BF16)
-    key_extra = ktab[...].reshape(nlon, LANES)
-    pad = jnp.zeros((LANES - 16, LANES), BF16)
-
-    def send_att(slot, peer, group):
-        index = slot * n_lon + peer
+    key_extra = ktab[...].reshape(nlon, LANES)[:, :16]
+    ones = jnp.ones((16, nlon), BF16)
+
+    row_work = Pairs(
+        lambda b, h: jnp.concatenate([keys[:, h // 4 * LANES:(h // 4 + 1) * LANES], key_extra], axis=1),
+        lambda b, h: jnp.concatenate(
+            [pair_of(queries_t[:, b * LANES:(b + 1) * LANES], h, size), extra1[b, h // 2]], axis=0
+        ),
+        None,
+        lambda b, h: jnp.concatenate([values_t[h * size:(h + 2) * size], ones], axis=0),
+        size,
+    )
+
+    distant_slot = slot_of(me_lat, (1 - side) * half)
+
+    def send_att(slot, peer):
+        group = distant_slot if slot < half else half + (n_lat - 2 - slot) % half
         return pltpu.make_async_remote_copy(
-            src_ref=att_out.at[index], dst_ref=att_in.at[group * rows + me_lon], send_sem=s3.at[0],
-            recv_sem=r3.at[group // half], device_id=(peer, lat_at(slot)), device_id_type=MESH,
-        )
-
-    units = [(b, h) for b in range(2) for h in range(0, heads, 2)]
-    row_work = Attention(
-        keys, key_extra, queries_t, lambda b, h: jnp.concatenate([extra1[b, h], pad], axis=0), values_t, size
-    )
+            src_ref=att_out.at[slot * n_lon + peer], dst_ref=att_in.at[group * rows + me_lon], send_sem=s3.at[0],
+            recv_sem=r3.at[min(slot // half, 1)], device_id=(peer, lat_at(slot)), device_id_type=MESH,
+        )
 
     def row_done(b, h):
         if h < heads - 2:
             return
-        att = row_work.taken(b, heads)
+        att = jnp.concatenate([row_work.held.pop((b, k)) for k in range(2, heads, 4)], axis=1)
         att_out[b * half * n_lon:(b + 1) * half * n_lon] = att.reshape(half * n_lon, cols, depth).astype(BF16)
         if b == 0:
             pl.semaphore_wait(plane_sem, n_lon - 1)
-            for step in range(half):
-                slot = step + (1 - side) * (half - 1 - 2 * step)
-                for hop in order + [0]:
-                    send_att(slot, partner(me_lon, hop, n_lon), own).start()
-        else:
-            for step in list(range(1, half)) + [0]:
-                for hop in order + [0]:
-                    if step or hop:
-                        slot = half + lax.rem(own + step, half)
-                        send_att(slot, partner(me_lon, hop, n_lon), half + own).start()
-
-    staggered(row_work.stages, units, row_done)
-    my_slot = (half + own) * rows + me_lon
-    att_in[pl.ds(my_slot, 1)] = att_out[pl.ds((half + own) * n_lon + me_lon, 1)]
+        for hop in order + [0]:
+            for slot in range(b * half, (b + 1) * half):
+                if hop or slot < n_lat - 1:
+                    send_att(slot, partner(me_lon, hop, n_lon)).start()
+
+    staggered(row_work.stages, [(b, h) for b in range(2) for h in range(0, heads, 2)], row_done)
+    att_in[pl.ds((n_lat - 1) * rows + me_lon, 1)] = att_out[pl.ds((n_lat - 1) * n_lon + me_lon, 1)]
 
     for name in ("wo1", "wq2", "wk2", "wv2", "wo2", "wg", "wu", "wd", "gain_lat", "gain_mlp"):
         loads[name].wait()
@@ -434,17 +496,58 @@
     near_all = whole(att_out.at[pl.ds(0, count // 2 - 1)], att_in.at[pl.ds(0, count // 2 - 1)], s3.at[0], r3.at[1])
     far_all = whole(att_out.at[pl.ds(0, count // 2)], att_in.at[pl.ds(0, count // 2)], s3.at[0], r3.at[0])
     att_all = whole(att_out.at[pl.ds(0, total - 1)], att_in.at[pl.ds(0, total - 1)], s3.at[0], r3.at[0])
+    starts = [list(range(cols)), list(range(cols // 2, cols)) + list(range(cols // 2))]
+
+    def by_column(f, values):
+        values = values.astype(F32).reshape(LANES, depth)
+        parts = []
+        for g in range(groups):
+            shuffle[groups * f + g] = values[:, g * LANES:(g + 1) * LANES]
+            parts.append([shuffle[groups * f + g, pl.ds(c, block, stride=cols), :] for c in starts[f]])
+        return jnp.concatenate([jnp.concatenate(part, axis=0) for part in parts], axis=1)
+
+    for f in range(2):
+        resid[f * LANES:(f + 1) * LANES] = by_column(f, field_in[f * half:(f + 1) * half])
+
+    firsts, keys2, queries2, turned2, values2 = {}, {}, {}, {}, {}
+
+    def project_columns(f):
+        attended = by_column(f, att_in[f * block:(f + 1) * block]).astype(BF16)
+        firsts[f] = resid[f * LANES:(f + 1) * LANES] + mm(attended, wo1[...])
+        gained = (firsts[f] * gain_lat[...]).astype(BF16)
+        factor = root_mean(firsts[f])
+        across = jnp.broadcast_to(factor, (LANES, LANES)).T[:1]
+        turned = jnp.broadcast_to(halves_turned(factor), (LANES, LANES)).T[:1]
+        keys2[f] = (mm(gained, wk2[...]) * factor).astype(BF16)
+        both_t = mm_nt(wqv2[...], gained)
+        queries2[f] = scaled_t(both_t[:depth], [one * across for one in scale_lat])
+        turned2[f] = scaled_t(mm_nt(wqv2[:depth], halves_turned(gained)), [one * turned for one in scale_lat])
+        values2[f] = (both_t[depth:] * across).astype(BF16)
+
     near_all.wait_recv()
+    project_columns(1)
     far_all.wait_recv()
-
-    resid = field_in[...].astype(F32).reshape(cells, depth)
-    attended = att_in[...].astype(F32).reshape(cells, depth).astype(BF16)
-    first = resid + mm(attended, wo1[...])
-    normed = normalize(first, gain_lat[...])
-    keys = mm(normed, wk2[...]).astype(BF16)
-    both_t = mm_nt(wqv2[...], normed)
-    queries_t = scaled_t(both_t[:depth], scale_lat)
-    values_t = both_t[depth:].astype(BF16)
+    project_columns(0)
+    part = LANES // 2
+    low = (iota((LANES, LANES), 1) < part).astype(F32).astype(BF16)
+    high = (iota((LANES, LANES), 1) >= part).astype(F32).astype(BF16)
+    ones = jnp.ones((16, LANES), BF16)
+
+    def column_keys(f, c, g):
+        lane = slice(g * LANES, (g + 1) * LANES)
+        return jnp.concatenate([keys2[c][:part, lane], keys2[1 - c][part:, lane]], axis=0)
+
+    def column_values(f, c, g):
+        row = slice(g * LANES, (g + 1) * LANES)
+        return jnp.concatenate([values2[c][row] * low + values2[1 - c][row] * high, ones], axis=0)
+
+    col_work = Quads(
+        column_keys,
+        lambda f, c, g: side_by_side(queries2[f], turned2[f], c if f == 0 else 1 - c, g, size),
+        lambda f, c, g: tables[f, c, g],
+        column_values,
+        size,
+    )
     ff = wg.shape[1]
     step_ff = min(ff, 256)
 
@@ -454,28 +557,37 @@
             device_id=(me_lon, lat_at(slot)), device_id_type=MESH,
         )
 
-    col_work = Attention(keys, onehot[...], queries_t, lambda b, h: extra2[b, h], values_t, size)
-
-    def col_done(b, h):
-        if h < heads - 2:
+    def col_done(f, c, g):
+        if c != (1 if f == 0 else 0) or g < groups - 1:
             return
-        second = first[b * LANES:(b + 1) * LANES] + mm(col_work.taken(b, heads).astype(BF16), wo2[...])
-        normed = normalize(second, gain_mlp[...])
-        for f in range(0, ff, step_ff):
-            gate = mm(normed, wg[:, f:f + step_ff])
-            upper = mm(normed, wu[:, f:f + step_ff])
-            hidden = (gate * (0.5 * jnp.tanh(0.5 * gate) + 0.5) * upper).astype(BF16)
-            second = second + mm(hidden, wd[f:f + step_ff, :])
-        upd_out[b * half:(b + 1) * half] = second.reshape(half, rows, cols, depth).astype(BF16)
-        if b == 0:
-            new = [send_upd(step + (1 - side) * (half - 1 - 2 * step)) for step in range(half)]
-        else:
-            new = [send_upd(half + lax.rem(own + step, half)) for step in range(1, half)]
-        for copy in new:
-            copy.start()
-
-    staggered(col_work.stages, units, col_done)
-    mine = pltpu.make_async_copy(upd_out.at[half + own], my_cols(out), s4.at[1])
+        att = jnp.concatenate(
+            [jnp.concatenate([col_work.held.pop((f, k, g)) for g in range(groups)], axis=1)
+             for k in ((0, 1) if f == 0 else (1, 0))], axis=0
+        )
+        second = firsts[f] + mm(att.astype(BF16), wo2[...])
+        gained = (second * gain_mlp[...]).astype(BF16)
+        factor = root_mean(second)
+        for k in range(0, ff, step_ff):
+            gate = mm(gained, wg[:, k:k + step_ff]) * factor
+            upper = mm(gained, wu[:, k:k + step_ff]) * factor
+            hidden[:, k:k + step_ff] = (gate * (0.5 * jnp.tanh(0.5 * gate) + 0.5) * upper).astype(BF16)
+        second = second + mm(hidden[...], wd[...])
+        for i, c in enumerate(starts[f]):
+            for g in range(groups):
+                shuffle[groups * f + g, pl.ds(c, block, stride=cols), :] = (
+                    second[i * block:(i + 1) * block, g * LANES:(g + 1) * LANES]
+                )
+        updated = jnp.concatenate([shuffle[groups * f + g] for g in range(groups)], axis=1)
+        upd_out[f * half:(f + 1) * half] = updated.reshape(half, rows, cols, depth).astype(BF16)
+        for slot in range(f * half, (f + 1) * half):
+            if slot < n_lat - 1:
+                send_upd(slot).start()
+
+    for f in range(2):
+        staggered(
+            col_work.stages, [(f, c, g) for c in ((0, 1) if f == 0 else (1, 0)) for g in range(groups)], col_done
+        )
+    mine = pltpu.make_async_copy(upd_out.at[n_lat - 1], my_cols(out), s4.at[1])
     mine.start()
     norm_all.wait_send()
     field_all.wait_send()
@@ -505,8 +617,8 @@
     ktab = np.zeros((nlon, LANES), np.float32)
     ktab[:, :8] = np.where(np.arange(8)[None] % 4 < 2, high, waves - high)
     ktab = ktab.astype(jnp.bfloat16).reshape(n_lat, n_lon * cols, LANES)
-    qtab = np.zeros((2, 16, LANES), np.float32)
-    qtab[:, :8] = waves.reshape(2, LANES, 8).transpose(0, 2, 1)
+    qtab = np.zeros((n_lat, 16, LANES), np.float32)
+    qtab[:, :8] = np.tile(waves.reshape(n_lat, LANES // 2, 8).transpose(0, 2, 1), (1, 1, 2))
     hbm = pl.BlockSpec(memory_space=pl.ANY)
     weights = (query_lon, key_lon, value_lon, out_lon, query_lat, key_lat, value_lat, out_lat,
                w_gate, w_up, w_down)
@@ -531,10 +643,12 @@
             pltpu.VMEM((n_lat, rows, cols, depth), BF16),
             pltpu.VMEM((2 * depth, depth), BF16),
             pltpu.VMEM((2 * depth, depth), BF16),
-            pltpu.VMEM((2, heads, 16, LANES), BF16),
-            pltpu.VMEM((2, heads, LANES, LANES), BF16),
-            pltpu.VMEM((cells, LANES), BF16),
-            dma((24,)),
+            pltpu.VMEM((2, heads // 2, 16, 2 * LANES), BF16),
+            pltpu.VMEM((2, 2, depth // LANES, LANES, 2 * LANES), F32),
+            pltpu.VMEM((cells, depth), F32),
+            pltpu.VMEM((2 * depth // LANES, LANES, LANES), F32),
+            pltpu.VMEM((LANES, w_gate.shape[1]), BF16),
+            dma((32,)),
             dma((1,)), dma((1,)),
             dma((1,)), dma((1,)),
             dma((1,)), dma((2,)),
@@ -554,8 +668,7 @@
 def fits(rows, width, n_lon, n_lat, heads, depth):
     return (
         rows == n_lon and n_lat % 2 == 0 and width == 8 * n_lat and rows * width == 2 * LANES
-        and width * n_lon == 2 * LANES and 2 * n_lat * rows + width // n_lat <= LANES
-        and LANES % (depth // heads) == 0 and LANES // (depth // heads) % 2 == 0
+        and width * n_lon == 2 * LANES and n_lat == 4 and depth % LANES == 0 and heads * LANES == 4 * depth
     )
 
 

time: 22.5 us -> 22.2 us (0.987)
  Pallas kernels: 21.7 us -> 21.4 us
    pallas_call x1, Pallas kernels: 21.7 us -> 21.4 us  [fused_body(): pl.pallas_call(functools.partial(block_kernel, n_lon, n_lat, rows, width,...]
where the time goes in v2:
time: 22.2 us; the launch traced here: 22 us
  Pallas kernels  21.4 us (96%)
  local copies, waits for them, and re-layouts  0.66 us (3%)
    pallas_call x1, Pallas kernels, fused_body(): pl.pallas_call(functools.partial(block_kernel, n_lon, n_lat, rows, width,...  21.4 us
    unnamed x1, local copies, waits for them, and re-layouts  0.66 us

profile of v2, /device:TPU:0, one launch (start us, length us, event | category | flops | bytes accessed | tf_op | source)
XLA Modules:
  0.0 22.0 jit_solution(13677599168709895192)
XLA Ops:
  0.0 21.4 %shard_map.199 = bf16[8,32,256]{2,1,0:T(8,128)(2,1)S(1)} custom-call(bf16[8,32,256]{2,1,0:T(8,128)(2,1)} %fields_h.1, f32[1,256]{1,0:T(1,128)} %bitcast.7, f32[1,256]{1,0:T(1,128)} %bitcast.8, f32[1,256]{1,0:T(1,128)} %bitcast.9, f32[1,8]{1,0:T(1,128)} %bitcast.10, f32[1,8]{1,0:T(1,128)} %bitcast.11, f32[1,8]{1,0:T(1,128)} %bitcast.12, f32[1,8]{1,0:T(1,128)} %bitcast.13, ...), custom_call_target="tpu_custom_call" | custom-call | tf_op jit(solution)/shard_map/pallas_call | solution.py:626
  21.4 0.7 %copy.23 = bf16[8,32,256]{2,1,0:T(8,128)(2,1)} copy(bf16[8,32,256]{2,1,0:T(8,128)(2,1)S(1)} %shard_map.199) | data formatting | bytes 262144

commit v3 on v2

--- a/solution.py
+++ b/solution.py
@@ -160,7 +160,7 @@
 
 
 def far_first(n):
-    return sorted(range(1, n), key=lambda step: -(2 * (step >> 1).bit_count() + (step & 1)))
+    return sorted(range(1, n), key=lambda step: (-(step >> 1).bit_count(), step & 1))
 
 
 def split_pairs(values, odd):
@@ -311,18 +311,22 @@
                 sem, inc=1, device_id=(partner(me_lon, step, n_lon), me_lat), device_id_type=MESH
             )
 
-    def signal_line(sem):
+    other = partner(me_lon, 1, n_lon)
+
+    def signal_line(sem, lons):
         @pl.when(me_lat > 0)
         def _():
-            pl.semaphore_signal(sem, inc=1, device_id=(me_lon, me_lat - 1), device_id_type=MESH)
+            for lon in lons:
+                pl.semaphore_signal(sem, inc=1, device_id=(lon, me_lat - 1), device_id_type=MESH)
 
         @pl.when(me_lat < n_lat - 1)
         def _():
-            pl.semaphore_signal(sem, inc=1, device_id=(me_lon, me_lat + 1), device_id_type=MESH)
+            for lon in lons:
+                pl.semaphore_signal(sem, inc=1, device_id=(lon, me_lat + 1), device_id_type=MESH)
 
     beside = jnp.minimum(me_lat, 1) + jnp.minimum(n_lat - 1 - me_lat, 1)
     signal_plane(barrier)
-    signal_line(barrier)
+    signal_line(barrier, (me_lon, other))
     for slot in range(n_lat):
         load(f"ktab{slot}", ktab_h.at[lat_at(slot)], ktab.at[slot])
         load(f"qtab{slot}", qtab_h.at[lat_at(slot)], qtab.at[slot])
@@ -345,7 +349,7 @@
         norm_out[:, pl.ds(slot_of(a, me_lat), 1)] = scaled[:, a:a + 1]
         field_out[a] = pieces[:, a]
 
-    pl.semaphore_wait(barrier, n_lon - 1 + beside)
+    pl.semaphore_wait(barrier, n_lon - 1 + 2 * beside)
 
     def my_cols(ref):
         return ref.at[:, pl.ds(pl.multiple_of(me_lat * cols, cols), cols), :]
@@ -361,7 +365,7 @@
         slot = slot_of(me_lat, peer)
         return pltpu.make_async_remote_copy(
             src_ref=field_out.at[peer], dst_ref=field_in.at[slot], send_sem=s2.at[0],
-            recv_sem=r2.at[0], device_id=(me_lon, peer), device_id_type=MESH,
+            recv_sem=r2.at[0], device_id=(other, peer), device_id_type=MESH,
         )
 
     def send_fields(hop):
@@ -381,15 +385,10 @@
 
     for step in order:
         send_norm(step).start()
-    for hop in range(1, n_lat):
-        if hop > 1:
-            pl.semaphore_wait(line_sem.at[hop - 1], beside)
-        if hop < n_lat - 1:
-            signal_line(line_sem.at[hop])
-        send_fields(hop)
-    signal_plane(plane_sem)
+    send_field(me_lat).start()
+    signal_line(line_sem.at[0], (me_lon,))
+    send_fields(1)
     norm_in[:, pl.ds(me_lon, 1)] = norm_out[pl.ds(me_lon, 1)].reshape(n_lat, 1, cols, depth)
-    field_in[n_lat - 1:] = field_out[pl.ds(me_lat, 1)]
 
     for name in ["wq1", "wk1", "wv1", "temp_lon", "bias_lon", "temp_lat", "bias_lat"] + [
         f"{kind}{slot}" for slot in range(n_lat) for kind in ("ktab", "qtab")
@@ -431,6 +430,25 @@
                 here = jnp.where(first_part, key_far, key_near) if c == 0 else jnp.where(first_part, key_near, key_far)
                 tables[f, c, g] = jnp.where(same, weight * jnp.abs(here - there).astype(F32), -1e30)
 
+    pl.semaphore_wait(line_sem.at[0], beside)
+
+    @pl.when(me_lat == 1)
+    def _():
+        pl.semaphore_signal(line_sem.at[1], inc=1, device_id=(me_lon, me_lat - 1), device_id_type=MESH)
+
+    @pl.when(me_lat == n_lat - 2)
+    def _():
+        pl.semaphore_signal(line_sem.at[1], inc=1, device_id=(me_lon, me_lat + 1), device_id_type=MESH)
+
+    send_fields(2)
+
+    @pl.when(beside < 2)
+    def _():
+        pl.semaphore_wait(line_sem.at[1], 1)
+
+    signal_plane(plane_sem)
+    send_fields(3)
+
     def scales(temp):
         return [jnp.broadcast_to(temp[:, h:h + 1] * (LOG2E / math.sqrt(size)), (size, LANES)) for h in range(heads)]
 
@@ -466,7 +484,7 @@
     def send_att(slot, peer):
         group = distant_slot if slot < half else half + (n_lat - 2 - slot) % half
         return pltpu.make_async_remote_copy(
-            src_ref=att_out.at[slot * n_lon + peer], dst_ref=att_in.at[group * rows + me_lon], send_sem=s3.at[0],
+            src_ref=att_out.at[slot * n_lon + partner(peer, 1, n_lon)], dst_ref=att_in.at[group * rows + me_lon], send_sem=s3.at[0],
             recv_sem=r3.at[min(slot // half, 1)], device_id=(peer, lat_at(slot)), device_id_type=MESH,
         )
 
@@ -483,14 +501,14 @@
                     send_att(slot, partner(me_lon, hop, n_lon)).start()
 
     staggered(row_work.stages, [(b, h) for b in range(2) for h in range(0, heads, 2)], row_done)
-    att_in[pl.ds((n_lat - 1) * rows + me_lon, 1)] = att_out[pl.ds((n_lat - 1) * n_lon + me_lon, 1)]
+    att_in[pl.ds((n_lat - 1) * rows + me_lon, 1)] = att_out[pl.ds((n_lat - 1) * n_lon + other, 1)]
 
     for name in ("wo1", "wq2", "wk2", "wv2", "wo2", "wg", "wu", "wd", "gain_lat", "gain_mlp"):
         loads[name].wait()
     wqv2[:depth] = wq2[...].T
     wqv2[depth:] = wv2[...].T
     scale_lat = scales(temp_lat)
-    field_all = whole(field_out.at[pl.ds(0, n_lat - 1)], field_in.at[pl.ds(0, n_lat - 1)], s2.at[0], r2.at[0])
+    field_all = whole(field_out, field_in, s2.at[0], r2.at[0])
     field_all.wait_recv()
 
     near_all = whole(att_out.at[pl.ds(0, count // 2 - 1)], att_in.at[pl.ds(0, count // 2 - 1)], s3.at[0], r3.at[1])
@@ -524,10 +542,10 @@
         turned2[f] = scaled_t(mm_nt(wqv2[:depth], halves_turned(gained)), [one * turned for one in scale_lat])
         values2[f] = (both_t[depth:] * across).astype(BF16)
 
+    far_all.wait_recv()
+    project_columns(0)
     near_all.wait_recv()
     project_columns(1)
-    far_all.wait_recv()
-    project_columns(0)
     part = LANES // 2
     low = (iota((LANES, LANES), 1) < part).astype(F32).astype(BF16)
     high = (iota((LANES, LANES), 1) >= part).astype(F32).astype(BF16)
@@ -554,7 +572,7 @@
     def send_upd(slot):
         return pltpu.make_async_remote_copy(
             src_ref=upd_out.at[slot], dst_ref=my_cols(out), send_sem=s4.at[0], recv_sem=r4.at[0],
-            device_id=(me_lon, lat_at(slot)), device_id_type=MESH,
+            device_id=(other, lat_at(slot)), device_id_type=MESH,
         )
 
     def col_done(f, c, g):
@@ -568,10 +586,10 @@
         gained = (second * gain_mlp[...]).astype(BF16)
         factor = root_mean(second)
         for k in range(0, ff, step_ff):
-            gate = mm(gained, wg[:, k:k + step_ff]) * factor
-            upper = mm(gained, wu[:, k:k + step_ff]) * factor
-            hidden[:, k:k + step_ff] = (gate * (0.5 * jnp.tanh(0.5 * gate) + 0.5) * upper).astype(BF16)
-        second = second + mm(hidden[...], wd[...])
+            gate = mm(gained, wg[:, k:k + step_ff])
+            upper = mm(gained, wu[:, k:k + step_ff])
+            hidden[:, k:k + step_ff] = (gate * upper * (jnp.tanh(gate * (0.5 * factor)) + 1.0)).astype(BF16)
+        second = second + (0.5 * factor * factor) * mm(hidden[...], wd[...])
         for i, c in enumerate(starts[f]):
             for g in range(groups):
                 shuffle[groups * f + g, pl.ds(c, block, stride=cols), :] = (
@@ -580,20 +598,16 @@
         updated = jnp.concatenate([shuffle[groups * f + g] for g in range(groups)], axis=1)
         upd_out[f * half:(f + 1) * half] = updated.reshape(half, rows, cols, depth).astype(BF16)
         for slot in range(f * half, (f + 1) * half):
-            if slot < n_lat - 1:
-                send_upd(slot).start()
+            send_upd(slot).start()
 
     for f in range(2):
         staggered(
             col_work.stages, [(f, c, g) for c in ((0, 1) if f == 0 else (1, 0)) for g in range(groups)], col_done
         )
-    mine = pltpu.make_async_copy(upd_out.at[n_lat - 1], my_cols(out), s4.at[1])
-    mine.start()
     norm_all.wait_send()
     field_all.wait_send()
     att_all.wait_send()
-    mine.wait()
-    upd_all = whole(upd_out.at[pl.ds(0, n_lat - 1)], upd_out.at[pl.ds(0, n_lat - 1)], s4.at[0], r4.at[0])
+    upd_all = whole(upd_out, upd_out, s4.at[0], r4.at[0])
     upd_all.wait_send()
     upd_all.wait_recv()
 
@@ -652,8 +666,8 @@
             dma((1,)), dma((1,)),
             dma((1,)), dma((1,)),
             dma((1,)), dma((2,)),
-            dma((2,)), dma((1,)),
-            pltpu.SemaphoreType.REGULAR((n_lat,)),
+            dma((1,)), dma((1,)),
+            pltpu.SemaphoreType.REGULAR((2,)),
             pltpu.SemaphoreType.REGULAR,
         ],
         compiler_params=pltpu.CompilerParams(collective_id=0, has_side_effects=True),

time: 22.2 us -> 21.4 us (0.964)
  the two profiles are of different devices: /device:TPU:0 before, /device:TPU:1 now
where the time goes in v3:
time: 21.4 us; the launch traced here: 21.2 us
  Pallas kernels  20.6 us (96%)
  local copies, waits for them, and re-layouts  0.66 us (3%)
    pallas_call x1, Pallas kernels, fused_body(): pl.pallas_call(functools.partial(block_kernel, n_lon, n_lat, rows, width,...  20.6 us
    unnamed x1, local copies, waits for them, and re-layouts  0.66 us

profile of v3, /device:TPU:1, one launch (start us, length us, event | category | flops | bytes accessed | tf_op | source)
XLA Modules:
  0.0 21.2 jit_solution(4764807733655846603)
XLA Ops:
  0.0 20.6 %shard_map.199 = bf16[8,32,256]{2,1,0:T(8,128)(2,1)S(1)} custom-call(bf16[8,32,256]{2,1,0:T(8,128)(2,1)} %fields_h.1, f32[1,256]{1,0:T(1,128)} %bitcast.7, f32[1,256]{1,0:T(1,128)} %bitcast.8, f32[1,256]{1,0:T(1,128)} %bitcast.9, f32[1,8]{1,0:T(1,128)} %bitcast.10, f32[1,8]{1,0:T(1,128)} %bitcast.11, f32[1,8]{1,0:T(1,128)} %bitcast.12, f32[1,8]{1,0:T(1,128)} %bitcast.13, ...), custom_call_target="tpu_custom_call" | custom-call | tf_op jit(solution)/shard_map/pallas_call | solution.py:640
  20.6 0.7 %copy.23 = bf16[8,32,256]{2,1,0:T(8,128)(2,1)} copy(bf16[8,32,256]{2,1,0:T(8,128)(2,1)S(1)} %shard_map.199) | data formatting | bytes 262144

commit v4 on v3

--- a/solution.py
+++ b/solution.py
@@ -500,7 +500,7 @@
                 if hop or slot < n_lat - 1:
                     send_att(slot, partner(me_lon, hop, n_lon)).start()
 
-    staggered(row_work.stages, [(b, h) for b in range(2) for h in range(0, heads, 2)], row_done)
+    staggered(row_work.stages, [(b, h) for b in (1, 0) for h in range(0, heads, 2)], row_done)
     att_in[pl.ds((n_lat - 1) * rows + me_lon, 1)] = att_out[pl.ds((n_lat - 1) * n_lon + other, 1)]
 
     for name in ("wo1", "wq2", "wk2", "wv2", "wo2", "wg", "wu", "wd", "gain_lat", "gain_mlp"):
@@ -542,10 +542,10 @@
         turned2[f] = scaled_t(mm_nt(wqv2[:depth], halves_turned(gained)), [one * turned for one in scale_lat])
         values2[f] = (both_t[depth:] * across).astype(BF16)
 
+    near_all.wait_recv()
+    project_columns(1)
     far_all.wait_recv()
     project_columns(0)
-    near_all.wait_recv()
-    project_columns(1)
     part = LANES // 2
     low = (iota((LANES, LANES), 1) < part).astype(F32).astype(BF16)
     high = (iota((LANES, LANES), 1) >= part).astype(F32).astype(BF16)

time: 21.4 us -> 21.2 us (level)
  the two profiles are of different devices: /device:TPU:1 before, /device:TPU:0 now
where the time goes in v4:
time: 21.2 us; the launch traced here: 20.9 us
  Pallas kernels  20.2 us (95%)
  local copies, waits for them, and re-layouts  0.66 us (3%)
    pallas_call x1, Pallas kernels, fused_body(): pl.pallas_call(functools.partial(block_kernel, n_lon, n_lat, rows, width,...  20.2 us
    unnamed x1, local copies, waits for them, and re-layouts  0.66 us

profile of v4, /device:TPU:0, one launch (start us, length us, event | category | flops | bytes accessed | tf_op | source)
XLA Modules:
  0.0 20.9 jit_solution(13436906732140590347)
XLA Ops:
  0.0 20.2 %shard_map.199 = bf16[8,32,256]{2,1,0:T(8,128)(2,1)S(1)} custom-call(bf16[8,32,256]{2,1,0:T(8,128)(2,1)} %fields_h.1, f32[1,256]{1,0:T(1,128)} %bitcast.7, f32[1,256]{1,0:T(1,128)} %bitcast.8, f32[1,256]{1,0:T(1,128)} %bitcast.9, f32[1,8]{1,0:T(1,128)} %bitcast.10, f32[1,8]{1,0:T(1,128)} %bitcast.11, f32[1,8]{1,0:T(1,128)} %bitcast.12, f32[1,8]{1,0:T(1,128)} %bitcast.13, ...), custom_call_target="tpu_custom_call" | custom-call | tf_op jit(solution)/shard_map/pallas_call | solution.py:640
  20.2 0.7 %copy.23 = bf16[8,32,256]{2,1,0:T(8,128)(2,1)} copy(bf16[8,32,256]{2,1,0:T(8,128)(2,1)S(1)} %shard_map.199) | data formatting | bytes 262144
